TPU v7x, 32 devices: a whole 2x2x4 slice. The times are simulated.
32 devices in a mesh: gx: 4 (over z), gy: 2 (over x), gz: 4 (over y, core).
Axes of the slice: x: 2, y: 2, z: 4, core: 2. Of those that a mesh axis runs over, the one named last changes fastest.
Arguments:
- images: float32 [2, 64, 64, 512], P(None, 'gx', 'gy', 'gz'), may hold values from -6 to 6
- velocity: float32 [2, 3, 8, 8, 64], P(None, None, 'gx', None, 'gz'), may hold values from -2 to 2
Outputs:
- new_velocity: float32 [2, 3, 8, 8, 64], P(None, None, 'gx', None, 'gz')
- velocity_field: bfloat16 [2, 3, 64, 64, 512], P(None, None, 'gx', 'gy', 'gz')
All inputs are finite; a program needn't handle non-finite values.
Results may differ from a plain program's by a relative error of at most 0.001.
Values sent between devices are 32-bit elements; how exact they have to be, the bound alone decides.
A program may use at most 64 MiB of HBM per device.

v0:
```python
import jax
import jax.numpy as jnp
from jax import lax
from jax.sharding import PartitionSpec as P

epsilon_value = 1e-05
step_size = 0.5


def extended_2(cells, sides, width):
    for axis, dim in sides:
        count = lax.axis_size(axis)
        ends = count - 1
        head = lax.slice_in_dim(cells, 0, width, axis=dim)
        tail = lax.slice_in_dim(cells, cells.shape[dim] - width, cells.shape[dim], axis=dim)
        cells = jnp.concatenate(
            [
                lax.ppermute(tail, axis, [(i, (i + 1) % count) for i in range(ends)]),
                cells,
                lax.ppermute(head, axis, [((i + 1) % count, i) for i in range(ends)]),
            ],
            axis=dim,
        )
    return cells


def spline_weight(offset):
    magnitude = jnp.abs(offset)
    interior = 2.0 / 3.0 - magnitude * magnitude + 0.5 * magnitude * magnitude * magnitude
    outside = jnp.maximum(2.0 - magnitude, 0.0)
    outside = outside * outside * outside / 6.0
    return jnp.where(magnitude < 1.0, interior, outside)


def spline_table(voxels, points, first_point):
    positions = jnp.arange(voxels, dtype=jnp.float32)[:, None]
    centres = 8.0 * (jnp.arange(points, dtype=jnp.float32)[None, :] + first_point) + 3.5
    return spline_weight((positions - centres) / 8.0)


def fold_matrix(length):
    table_rows = jnp.arange(length, dtype=jnp.int32)[:, None]
    columns = jnp.arange(length - 8, dtype=jnp.int32)[None, :]
    matches = (
        (table_rows == columns + 4)
        | (table_rows < 2) & (columns == table_rows)
        | (table_rows >= length - 2) & (columns == table_rows - 8)
    )
    return matches.astype(jnp.float32)


def window_sum(values, which_axis, keep_count):
    running = lax.slice_in_dim(values, 0, keep_count, axis=which_axis)
    for offset in range(1, 9):
        running = running + lax.slice_in_dim(values, offset, offset + keep_count, axis=which_axis)
    return running


def gradient(volume, count_x, count_y, count_z):
    along_x = (
        volume[5 : 5 + count_x, 4 : 4 + count_y, 4 : 4 + count_z]
        - volume[3 : 3 + count_x, 4 : 4 + count_y, 4 : 4 + count_z]
    )
    along_y = (
        volume[4 : 4 + count_x, 5 : 5 + count_y, 4 : 4 + count_z]
        - volume[4 : 4 + count_x, 3 : 3 + count_y, 4 : 4 + count_z]
    )
    along_z = (
        volume[4 : 4 + count_x, 4 : 4 + count_y, 5 : 5 + count_z]
        - volume[4 : 4 + count_x, 4 : 4 + count_y, 3 : 3 + count_z]
    )
    return 0.5 * jnp.stack([along_x, along_y, along_z])


def local_forces(padded):
    count_x = padded.shape[1] - 8
    count_y = padded.shape[2] - 8
    count_z = padded.shape[3] - 8
    fixed_side = padded[0]
    moving_side = padded[1]
    products = jnp.stack(
        [
            fixed_side,
            moving_side,
            fixed_side * fixed_side,
            moving_side * moving_side,
            fixed_side * moving_side,
        ]
    )
    window_sums = window_sum(window_sum(window_sum(products, 1, count_x), 2, count_y), 3, count_z)
    averages = window_sums / 729.0
    mean_fixed = averages[0]
    mean_moving = averages[1]
    var_fixed = averages[2] - mean_fixed * mean_fixed + epsilon_value
    var_moving = averages[3] - mean_moving * mean_moving + epsilon_value
    covariance = averages[4] - mean_fixed * mean_moving
    centre_fixed = fixed_side[4 : 4 + count_x, 4 : 4 + count_y, 4 : 4 + count_z] - mean_fixed
    centre_moving = moving_side[4 : 4 + count_x, 4 : 4 + count_y, 4 : 4 + count_z] - mean_moving
    factor = 2.0 * covariance / (var_fixed * var_moving)
    pull_fixed = factor * (centre_moving - covariance / var_fixed * centre_fixed)
    pull_moving = factor * (centre_fixed - covariance / var_moving * centre_moving)
    return jnp.stack(
        [
            pull_fixed[None] * gradient(fixed_side, count_x, count_y, count_z),
            pull_moving[None] * gradient(moving_side, count_x, count_y, count_z),
        ]
    )


def shards(images, velocity):
    highest = lax.Precision.HIGHEST
    count_x = images.shape[1]
    count_y = images.shape[2]
    count_z = images.shape[3]
    block_x = count_x // 8
    block_y = count_y // 8
    block_z = count_z // 8
    padded = extended_2(images, (("gx", 1), ("gy", 2), ("gz", 3)), 4)
    pushes = local_forces(padded)
    table_x = spline_table(count_x, block_x + 4, -2.0)
    table_y = spline_table(count_y, block_y + 4, -2.0)
    table_z = spline_table(count_z, block_z + 4, -2.0)
    along_z = jnp.einsum("hcxyz,zk->hcxyk", pushes, table_z, precision=highest)
    along_y = jnp.einsum("hcxyk,yj->hcxjk", along_z, table_y, precision=highest)
    partial_value = jnp.einsum("hcxjk,xi->hcijk", along_y, table_x, precision=highest)
    fold_x = fold_matrix(block_x + 8)
    fold_z = fold_matrix(block_z + 8)
    extended = extended_2(partial_value, (("gx", 2), ("gz", 4)), 2)
    folded = jnp.einsum("hcpqr,pi->hciqr", extended, fold_x, precision=highest)
    folded = jnp.einsum("hciqr,rk->hciqk", folded, fold_z, precision=highest)
    whole_rows = block_y * lax.axis_size("gy") + 4
    canvas = jnp.zeros((2, 3, block_x, whole_rows, block_z), jnp.float32)
    canvas = lax.dynamic_update_slice_in_dim(canvas, folded, lax.axis_index("gy") * block_y, 3)
    summed = lax.psum(canvas, "gy")
    descent = summed[:, :, :, 2 : whole_rows - 2, :]
    new_velocity = velocity + step_size * descent
    beside_all = extended_2(new_velocity, (("gx", 2), ("gz", 4)), 2)
    rows_padded = jnp.pad(beside_all, ((0, 0), (0, 0), (0, 0), (2, 2), (0, 0)))
    window = lax.dynamic_slice_in_dim(rows_padded, lax.axis_index("gy") * block_y, block_y + 4, 3)
    field_x = jnp.einsum("hcijk,xi->hcxjk", window, table_x, precision=highest)
    field_y = jnp.einsum("hcxjk,yj->hcxyk", field_x, table_y, precision=highest)
    velocity_field = jnp.einsum("hcxyk,zk->hcxyz", field_y, table_z, precision=highest).astype(
        jnp.bfloat16
    )
    return (new_velocity, velocity_field)


def solution(mesh):
    placed = (P(None, "gx", "gy", "gz"), P(None, None, "gx", None, "gz"))
    return jax.shard_map(
        shards,
        mesh=mesh,
        in_specs=placed,
        out_specs=(P(None, None, "gx", None, "gz"), P(None, None, "gx", "gy", "gz")),
        check_vma=False,
    )
```

profile of v0, /device:TPU:1, one launch (start us, length us, event | category | flops | bytes accessed | tf_op | source)
XLA Modules:
  0.0 113.0 jit_solution(16727576706066880578)
XLA Ops:
  0.6 1.0 fusion.202
  1.6 4.0 %collective-permute-start = (f32[2,4,32,128]{3,2,1,0:T(8,128)S(1)}, f32[2,4,32,128]{3,2,1,0:T(8,128)S(1)}, u32[]{:S(2)}, u32[]{:S(2)}) collective-permute-start(f32[2,4,32,128]{3,2,1,0:T(8,128)S(1)} %get-tuple-element.25), channel_id=1, source_target_pairs={{0,8},{8,16},{16,24},{1,9},{9,17},{17,25},{2,10},{10,18},{18,26},{... | collective-permute-start | bytes 393224 | tf_op jit(solution)/shard_map/ppermute | solution.py:18
  5.7 1.3 %collective-permute-start.1 = (f32[2,4,32,128]{3,2,1,0:T(8,128)S(1)}, f32[2,4,32,128]{3,2,1,0:T(8,128)S(1)}, u32[]{:S(2)}, u32[]{:S(2)}) collective-permute-start(f32[2,4,32,128]{3,2,1,0:T(8,128)S(1)} %get-tuple-element.24), channel_id=1, source_target_pairs={{8,0},{16,8},{24,16},{9,1},{17,9},{25,17},{10,2},{18,10},{26,18},{... | collective-permute-start | bytes 393224 | tf_op jit(solution)/shard_map/ppermute | solution.py:20
  7.0 0.8 collective-permute-done
  7.8 1.1 constant_dynamic-update-slice_fusion.1
  8.9 2.5 %collective-permute-done.1 = f32[2,4,32,128]{3,2,1,0:T(8,128)S(1)} collective-permute-done((f32[2,4,32,128]{3,2,1,0:T(8,128)S(1)}, f32[2,4,32,128]{3,2,1,0:T(8,128)S(1)}, u32[]{:S(2)}, u32[]{:S(2)}) %collective-permute-start.1) | collective-permute-done | bytes 131104 | tf_op jit(solution)/shard_map/ppermute | solution.py:20
  11.4 3.1 %collective-permute-start.2 = (f32[2,24,4,128]{3,1,2,0:T(8,128)S(1)}, f32[2,24,4,128]{3,1,2,0:T(8,128)S(1)}, u32[]{:S(2)}, u32[]{:S(2)}) collective-permute-start(f32[2,24,4,128]{3,1,2,0:T(8,128)S(1)} %copy.59), channel_id=1, source_target_pairs={{0,4},{1,5},{2,6},{3,7},{8,12},{9,13},{10,14},{11,15},{16,20},{17,... | collective-permute-start | bytes 294920 | tf_op jit(solution)/shard_map/ppermute | solution.py:18
  14.6 1.3 %collective-permute-start.3 = (f32[2,24,4,128]{3,1,2,0:T(8,128)S(1)}, f32[2,24,4,128]{3,1,2,0:T(8,128)S(1)}, u32[]{:S(2)}, u32[]{:S(2)}) collective-permute-start(f32[2,24,4,128]{3,1,2,0:T(8,128)S(1)} %copy.60), channel_id=1, source_target_pairs={{4,0},{5,1},{6,2},{7,3},{12,8},{13,9},{14,10},{15,11},{20,16},{21,... | collective-permute-start | bytes 294920 | tf_op jit(solution)/shard_map/ppermute | solution.py:20
  15.9 0.3 collective-permute-done.2
  16.2 3.7 %collective-permute-done.3 = f32[2,24,4,128]{3,1,2,0:T(8,128)S(1)} collective-permute-done((f32[2,24,4,128]{3,1,2,0:T(8,128)S(1)}, f32[2,24,4,128]{3,1,2,0:T(8,128)S(1)}, u32[]{:S(2)}, u32[]{:S(2)}) %collective-permute-start.3) | collective-permute-done | bytes 98336 | tf_op jit(solution)/shard_map/ppermute | solution.py:20
  20.0 0.1 pad_maximum_fusion.2
  20.1 0.3 fusion.200
  20.4 0.4 copy.44
  20.8 6.6 %collective-permute-start.4 = (f32[2,24,40,4]{2,1,3,0:T(8,128)S(1)}, f32[2,24,40,4]{2,1,3,0:T(8,128)S(1)}, u32[]{:S(2)}, u32[]{:S(2)}) collective-permute-start(f32[2,24,40,4]{2,1,3,0:T(8,128)S(1)} %copy.44), channel_id=1, source_target_pairs={{0,1},{1,2},{2,3},{4,5},{5,6},{6,7},{8,9},{9,10},{10,11},{12,13},{... | collective-permute-start | bytes 92168 | tf_op jit(solution)/shard_map/ppermute | solution.py:18
  27.4 0.4 copy.45
  27.8 1.9 %collective-permute-start.5 = (f32[2,24,40,4]{2,1,3,0:T(8,128)S(1)}, f32[2,24,40,4]{2,1,3,0:T(8,128)S(1)}, u32[]{:S(2)}, u32[]{:S(2)}) collective-permute-start(f32[2,24,40,4]{2,1,3,0:T(8,128)S(1)} %copy.45), channel_id=1, source_target_pairs={{1,0},{2,1},{3,2},{5,4},{6,5},{7,6},{9,8},{10,9},{11,10},{13,12},{... | collective-permute-start | bytes 92168 | tf_op jit(solution)/shard_map/ppermute | solution.py:20
  29.8 0.0 collective-permute-done.4
  29.8 0.4 copy.46
  30.2 3.6 %collective-permute-done.5 = f32[2,24,40,4]{2,1,3,0:T(8,128)S(1)} collective-permute-done((f32[2,24,40,4]{2,1,3,0:T(8,128)S(1)}, f32[2,24,40,4]{2,1,3,0:T(8,128)S(1)}, u32[]{:S(2)}, u32[]{:S(2)}) %collective-permute-start.5) | collective-permute-done | bytes 30752 | tf_op jit(solution)/shard_map/ppermute | solution.py:20
  33.7 0.4 copy.47
  34.2 1.0 pad_maximum_fusion.1
  35.2 0.4 slice_bitcast_fusion.1
  35.6 1.8 %pad_maximum_fusion = f32[5,24,40,136]{3,2,1,0:T(8,128)S(1)} fusion(f32[1,24,40,136]{3,2,1,0:T(8,128)S(1)} %get-tuple-element.12, f32[1,24,40,136]{3,2,1,0:T(8,128)S(1)} %get-tuple-element.14, f32[1,24,40,136]{3,2,1,0:T(8,128)S(1)} %get-tuple-element.11, f32[2,24,40,4]{3,2,1,0:T(8,128)S(1)} %copy.47, f32[2,24,4,128]{3,2,1,0:T(4,128)S(1)} %copy.43, ...), kind=kLoop, calls=%fused_computation | loop fusion | flops 4569600 | bytes 5222400 | tf_op jit(solution)/shard_map/stack | solution.py:81
  37.4 3.0 %slice_add_fusion = f32[5,16,40,136]{3,2,1,0:T(8,128)S(1)} fusion(f32[5,24,40,136]{3,2,1,0:T(8,128)S(1)} %pad_maximum_fusion), kind=kLoop, calls=%fused_computation.1 | loop fusion | flops 3481600 | bytes 17408000 | tf_op jit(solution)/shard_map/add | solution.py:55
  40.5 2.0 %slice_add_fusion.8 = f32[5,16,32,136]{3,2,1,0:T(8,128)S(1)} fusion(f32[5,16,40,136]{3,2,1,0:T(8,128)S(1)} %slice_add_fusion), kind=kLoop, calls=%fused_computation.9 | loop fusion | flops 2785280 | bytes 13926400 | tf_op jit(solution)/shard_map/add | solution.py:55
  42.4 2.8 %fusion.4 = f32[5,16,32,128]{3,2,1,0:T(8,128)S(1)} fusion(f32[5,16,32,136]{3,2,1,0:T(8,128)S(1)} %slice_add_fusion.8), kind=kLoop, calls=%fused_computation.25 | loop fusion | flops 2949120 | bytes 13107200 | tf_op jit(solution)/shard_map/div | solution.py:91
  45.2 0.6 fusion.18
  45.8 0.5 multiply_multiply_fusion.1
  46.3 0.1 maximum_multiply_fusion
  46.4 0.1 maximum_multiply_fusion.1
  46.5 6.2 %fusion = f32[2,3,16,32,20]{3,4,2,1,0:T(8,128)S(1)} fusion(f32[1,3,16,32,128]{4,3,2,1,0:T(8,128)S(1)} %maximum_multiply_fusion.1, f32[1,3,16,32,128]{4,3,2,1,0:T(8,128)S(1)} %maximum_multiply_fusion, f32[20]{0:T(128)S(1)} %multiply_add_fusion), kind=kOutput, calls=%fused_computation.18 | convolution fusion | flops 94806016 | bytes 1818704 | tf_op jit(solution)/shard_map/hcxyz,zk->hcxyk/dot_general | solution.py:123
  52.7 5.9 %convolution_bitcast_fusion.2 = f32[2,3,16,8,20]{4,3,2,1,0:T(8,128)S(1)} fusion(f32[2,3,16,32,20]{3,4,2,1,0:T(8,128)S(1)} %fusion, f32[8]{0:T(128)S(1)} %multiply_add_fusion.1), kind=kOutput, calls=%fused_computation.34 | convolution fusion | flops 5902336 | bytes 307232 | tf_op jit(solution)/shard_map/hcxyk,yj->hcxjk/dot_general | solution.py:124
  58.6 0.0 copy-start
  58.6 0.4 convolution_bitcast_fusion.3
  59.1 3.2 %collective-permute-start.6 = (f32[2,3,2,8,20]{4,2,3,1,0:T(2,128)S(1)}, f32[2,3,2,8,20]{4,2,3,1,0:T(2,128)S(1)}, u32[]{:S(2)}, u32[]{:S(2)}) collective-permute-start(f32[2,3,2,8,20]{4,2,3,1,0:T(2,128)S(1)} %get-tuple-element.30), channel_id=1, source_target_pairs={{0,8},{8,16},{16,24},{1,9},{9,17},{17,25},{2,10},{10,18},{18,26},{... | collective-permute-start | bytes 23048 | tf_op jit(solution)/shard_map/ppermute | solution.py:18
  62.3 1.5 %collective-permute-start.7 = (f32[2,3,2,8,20]{4,2,3,1,0:T(2,128)S(1)}, f32[2,3,2,8,20]{4,2,3,1,0:T(2,128)S(1)}, u32[]{:S(2)}, u32[]{:S(2)}) collective-permute-start(f32[2,3,2,8,20]{4,2,3,1,0:T(2,128)S(1)} %get-tuple-element.31), channel_id=1, source_target_pairs={{8,0},{16,8},{24,16},{9,1},{17,9},{25,17},{10,2},{18,10},{26,18},{... | collective-permute-start | bytes 23048 | tf_op jit(solution)/shard_map/ppermute | solution.py:20
  63.8 0.0 collective-permute-done.6
  63.8 3.3 %collective-permute-done.7 = f32[2,3,2,8,20]{4,2,3,1,0:T(2,128)S(1)} collective-permute-done((f32[2,3,2,8,20]{4,2,3,1,0:T(2,128)S(1)}, f32[2,3,2,8,20]{4,2,3,1,0:T(2,128)S(1)}, u32[]{:S(2)}, u32[]{:S(2)}) %collective-permute-start.7) | collective-permute-done | bytes 7712 | tf_op jit(solution)/shard_map/ppermute | solution.py:20
  67.1 0.1 pad_maximum_fusion.3
  67.2 0.2 fusion.203
  67.4 3.3 %collective-permute-start.8 = (f32[2,3,10,8,2]{4,2,3,1,0:T(8,128)S(1)}, f32[2,3,10,8,2]{4,2,3,1,0:T(8,128)S(1)}, u32[]{:S(2)}, u32[]{:S(2)}) collective-permute-start(f32[2,3,10,8,2]{4,2,3,1,0:T(8,128)S(1)} %get-tuple-element.26), channel_id=1, source_target_pairs={{0,1},{1,2},{2,3},{4,5},{5,6},{6,7},{8,9},{9,10},{10,11},{12,13},{... | collective-permute-start | bytes 11528 | tf_op jit(solution)/shard_map/ppermute | solution.py:18
  70.6 1.9 %collective-permute-start.9 = (f32[2,3,10,8,2]{4,2,3,1,0:T(8,128)S(1)}, f32[2,3,10,8,2]{4,2,3,1,0:T(8,128)S(1)}, u32[]{:S(2)}, u32[]{:S(2)}) collective-permute-start(f32[2,3,10,8,2]{4,2,3,1,0:T(8,128)S(1)} %get-tuple-element.27), channel_id=1, source_target_pairs={{1,0},{2,1},{3,2},{5,4},{6,5},{7,6},{9,8},{10,9},{11,10},{13,12},{... | collective-permute-start | bytes 11528 | tf_op jit(solution)/shard_map/ppermute | solution.py:20
  72.6 2.8 %collective-permute-done.8 = f32[2,3,10,8,2]{4,2,3,1,0:T(8,128)S(1)} collective-permute-done((f32[2,3,10,8,2]{4,2,3,1,0:T(8,128)S(1)}, f32[2,3,10,8,2]{4,2,3,1,0:T(8,128)S(1)}, u32[]{:S(2)}, u32[]{:S(2)}) %collective-permute-start.8) | collective-permute-done | bytes 3872 | tf_op jit(solution)/shard_map/ppermute | solution.py:18
  75.3 4.7 %collective-permute-done.9 = f32[2,3,10,8,2]{4,2,3,1,0:T(8,128)S(1)} collective-permute-done((f32[2,3,10,8,2]{4,2,3,1,0:T(8,128)S(1)}, f32[2,3,10,8,2]{4,2,3,1,0:T(8,128)S(1)}, u32[]{:S(2)}, u32[]{:S(2)}) %collective-permute-start.9) | collective-permute-done | bytes 3872 | tf_op jit(solution)/shard_map/ppermute | solution.py:20
  80.0 0.6 convolution_bitcast_fusion.4
  80.6 0.2 fusion.52
  80.9 5.6 %psum.7 = f32[2,3,2,12,16]{4,2,3,1,0:T(2,128)S(1)} all-reduce(f32[2,3,2,12,16]{4,2,3,1,0:T(2,128)S(1)} %copy_dynamic-update-slice_fusion), channel_id=1, replica_groups=mesh['gx'=4,'gy'=2,'gz'=4] {'gy'}, use_global_device_ids=true, to_apply=%region_0.1 | all-reduce | flops 2304 | bytes 18432 | tf_op jit(solution)/shard_map/psum | solution.py:134
  86.5 0.0 copy-done
  86.6 3.2 %collective-permute-start.10 = (f32[2,3,2,8,16]{4,2,3,1,0:T(2,128)S(1)}, f32[2,3,2,8,16]{4,2,3,1,0:T(2,128)S(1)}, u32[]{:S(2)}, u32[]{:S(2)}) collective-permute-start(f32[2,3,2,8,16]{4,2,3,1,0:T(2,128)S(1)} %fusion.51), channel_id=1, source_target_pairs={{0,8},{8,16},{16,24},{1,9},{9,17},{17,25},{2,10},{10,18},{18,26},{... | collective-permute-start | bytes 18440 | tf_op jit(solution)/shard_map/ppermute | solution.py:18
  89.8 1.3 %collective-permute-start.11 = (f32[2,3,2,8,16]{4,2,3,1,0:T(2,128)S(1)}, f32[2,3,2,8,16]{4,2,3,1,0:T(2,128)S(1)}, u32[]{:S(2)}, u32[]{:S(2)}) collective-permute-start(f32[2,3,2,8,16]{4,2,3,1,0:T(2,128)S(1)} %fusion.51), channel_id=1, source_target_pairs={{8,0},{16,8},{24,16},{9,1},{17,9},{25,17},{10,2},{18,10},{26,18},{... | collective-permute-start | bytes 18440 | tf_op jit(solution)/shard_map/ppermute | solution.py:20
  91.1 0.0 collective-permute-done.10
  91.1 3.5 %collective-permute-done.11 = f32[2,3,2,8,16]{4,2,3,1,0:T(2,128)S(1)} collective-permute-done((f32[2,3,2,8,16]{4,2,3,1,0:T(2,128)S(1)}, f32[2,3,2,8,16]{4,2,3,1,0:T(2,128)S(1)}, u32[]{:S(2)}, u32[]{:S(2)}) %collective-permute-start.11) | collective-permute-done | bytes 6176 | tf_op jit(solution)/shard_map/ppermute | solution.py:20
  94.6 0.1 pad_maximum_fusion.4
  94.7 0.1 fusion.204
  94.8 4.6 %collective-permute-start.12 = (f32[2,3,6,8,2]{4,2,3,1,0:T(8,128)S(1)}, f32[2,3,6,8,2]{4,2,3,1,0:T(8,128)S(1)}, u32[]{:S(2)}, u32[]{:S(2)}) collective-permute-start(f32[2,3,6,8,2]{4,2,3,1,0:T(8,128)S(1)} %get-tuple-element.29), channel_id=1, source_target_pairs={{0,1},{1,2},{2,3},{4,5},{5,6},{6,7},{8,9},{9,10},{10,11},{12,13},{... | collective-permute-start | bytes 6920 | tf_op jit(solution)/shard_map/ppermute | solution.py:18
  99.4 1.9 %collective-permute-start.13 = (f32[2,3,6,8,2]{4,2,3,1,0:T(8,128)S(1)}, f32[2,3,6,8,2]{4,2,3,1,0:T(8,128)S(1)}, u32[]{:S(2)}, u32[]{:S(2)}) collective-permute-start(f32[2,3,6,8,2]{4,2,3,1,0:T(8,128)S(1)} %get-tuple-element.28), channel_id=1, source_target_pairs={{1,0},{2,1},{3,2},{5,4},{6,5},{7,6},{9,8},{10,9},{11,10},{13,12},{... | collective-permute-start | bytes 6920 | tf_op jit(solution)/shard_map/ppermute | solution.py:20
  101.4 0.6 copy.53
  102.0 0.0 collective-permute-done.12
  102.0 4.4 %collective-permute-done.13 = f32[2,3,6,8,2]{4,2,3,1,0:T(8,128)S(1)} collective-permute-done((f32[2,3,6,8,2]{4,2,3,1,0:T(8,128)S(1)}, f32[2,3,6,8,2]{4,2,3,1,0:T(8,128)S(1)}, u32[]{:S(2)}, u32[]{:S(2)}) %collective-permute-start.13) | collective-permute-done | bytes 2336 | tf_op jit(solution)/shard_map/ppermute | solution.py:20
  106.4 0.9 convolution_bitcast_fusion.1
  107.4 2.1 %convolution_bitcast_fusion = f32[2,3,16,32,20]{3,4,2,1,0:T(8,128)S(1)} fusion(f32[2,3,16,8,20]{4,2,3,1,0:T(8,128)S(1)} %convolution_bitcast_fusion.1, f32[8]{0:T(128)S(1)} %multiply_add_fusion.1), kind=kOutput, calls=%fused_computation.23 | convolution fusion | flops 5902336 | bytes 307232 | tf_op jit(solution)/shard_map/hcxjk,yj->hcxyk/dot_general | solution.py:141
  109.4 3.6 %convolution_convert_fusion = bf16[2,3,16,32,128]{4,3,2,1,0:T(8,128)(2,1)} fusion(f32[2,3,16,32,20]{3,4,2,1,0:T(8,128)S(1)} %convolution_bitcast_fusion, f32[20]{0:T(128)S(1)} %multiply_add_fusion), kind=kOutput, calls=%fused_computation.22 | convolution fusion | flops 94806016 | bytes 1032272 | tf_op jit(solution)/shard_map/hcxyk,zk->hcxyz/dot_general | solution.py:142
  (21 shorter events, 0.4 us)
Async XLA Ops:
  1.6 6.2 %collective-permute-start = (f32[2,4,32,128]{3,2,1,0:T(8,128)S(1)}, f32[2,4,32,128]{3,2,1,0:T(8,128)S(1)}, u32[]{:S(2)}, u32[]{:S(2)}) collective-permute-start(f32[2,4,32,128]{3,2,1,0:T(8,128)S(1)} %get-tuple-element.25), channel_id=1, source_target_pairs={{0,8},{8,16},{16,24},{1,9},{9,17},{17,25},{2,10},{10,18},{18,26},{... | collective-permute-start | bytes 393224 | tf_op jit(solution)/shard_map/ppermute | solution.py:18
  5.7 5.7 %collective-permute-start.1 = (f32[2,4,32,128]{3,2,1,0:T(8,128)S(1)}, f32[2,4,32,128]{3,2,1,0:T(8,128)S(1)}, u32[]{:S(2)}, u32[]{:S(2)}) collective-permute-start(f32[2,4,32,128]{3,2,1,0:T(8,128)S(1)} %get-tuple-element.24), channel_id=1, source_target_pairs={{8,0},{16,8},{24,16},{9,1},{17,9},{25,17},{10,2},{18,10},{26,18},{... | collective-permute-start | bytes 393224 | tf_op jit(solution)/shard_map/ppermute | solution.py:20
  11.4 4.7 %collective-permute-start.2 = (f32[2,24,4,128]{3,1,2,0:T(8,128)S(1)}, f32[2,24,4,128]{3,1,2,0:T(8,128)S(1)}, u32[]{:S(2)}, u32[]{:S(2)}) collective-permute-start(f32[2,24,4,128]{3,1,2,0:T(8,128)S(1)} %copy.59), channel_id=1, source_target_pairs={{0,4},{1,5},{2,6},{3,7},{8,12},{9,13},{10,14},{11,15},{16,20},{17,... | collective-permute-start | bytes 294920 | tf_op jit(solution)/shard_map/ppermute | solution.py:18
  14.6 5.4 %collective-permute-start.3 = (f32[2,24,4,128]{3,1,2,0:T(8,128)S(1)}, f32[2,24,4,128]{3,1,2,0:T(8,128)S(1)}, u32[]{:S(2)}, u32[]{:S(2)}) collective-permute-start(f32[2,24,4,128]{3,1,2,0:T(8,128)S(1)} %copy.60), channel_id=1, source_target_pairs={{4,0},{5,1},{6,2},{7,3},{12,8},{13,9},{14,10},{15,11},{20,16},{21,... | collective-permute-start | bytes 294920 | tf_op jit(solution)/shard_map/ppermute | solution.py:20
  20.8 8.9 %collective-permute-start.4 = (f32[2,24,40,4]{2,1,3,0:T(8,128)S(1)}, f32[2,24,40,4]{2,1,3,0:T(8,128)S(1)}, u32[]{:S(2)}, u32[]{:S(2)}) collective-permute-start(f32[2,24,40,4]{2,1,3,0:T(8,128)S(1)} %copy.44), channel_id=1, source_target_pairs={{0,1},{1,2},{2,3},{4,5},{5,6},{6,7},{8,9},{9,10},{10,11},{12,13},{... | collective-permute-start | bytes 92168 | tf_op jit(solution)/shard_map/ppermute | solution.py:18
  27.8 5.9 %collective-permute-start.5 = (f32[2,24,40,4]{2,1,3,0:T(8,128)S(1)}, f32[2,24,40,4]{2,1,3,0:T(8,128)S(1)}, u32[]{:S(2)}, u32[]{:S(2)}) collective-permute-start(f32[2,24,40,4]{2,1,3,0:T(8,128)S(1)} %copy.45), channel_id=1, source_target_pairs={{1,0},{2,1},{3,2},{5,4},{6,5},{7,6},{9,8},{10,9},{11,10},{13,12},{... | collective-permute-start | bytes 92168 | tf_op jit(solution)/shard_map/ppermute | solution.py:20
  58.6 27.9 %copy-start = (f32[2,3,2,8,16]{4,3,2,1,0:T(8,128)S(1)}, f32[2,3,2,8,16]{4,3,2,1,0:T(8,128)}, u32[]{:S(2)}) copy-start(f32[2,3,2,8,16]{4,3,2,1,0:T(8,128)} %param.3) | copy-start | bytes 18436
  59.1 4.7 %collective-permute-start.6 = (f32[2,3,2,8,20]{4,2,3,1,0:T(2,128)S(1)}, f32[2,3,2,8,20]{4,2,3,1,0:T(2,128)S(1)}, u32[]{:S(2)}, u32[]{:S(2)}) collective-permute-start(f32[2,3,2,8,20]{4,2,3,1,0:T(2,128)S(1)} %get-tuple-element.30), channel_id=1, source_target_pairs={{0,8},{8,16},{16,24},{1,9},{9,17},{17,25},{2,10},{10,18},{18,26},{... | collective-permute-start | bytes 23048 | tf_op jit(solution)/shard_map/ppermute | solution.py:18
  62.3 4.8 %collective-permute-start.7 = (f32[2,3,2,8,20]{4,2,3,1,0:T(2,128)S(1)}, f32[2,3,2,8,20]{4,2,3,1,0:T(2,128)S(1)}, u32[]{:S(2)}, u32[]{:S(2)}) collective-permute-start(f32[2,3,2,8,20]{4,2,3,1,0:T(2,128)S(1)} %get-tuple-element.31), channel_id=1, source_target_pairs={{8,0},{16,8},{24,16},{9,1},{17,9},{25,17},{10,2},{18,10},{26,18},{... | collective-permute-start | bytes 23048 | tf_op jit(solution)/shard_map/ppermute | solution.py:20
  67.4 8.0 %collective-permute-start.8 = (f32[2,3,10,8,2]{4,2,3,1,0:T(8,128)S(1)}, f32[2,3,10,8,2]{4,2,3,1,0:T(8,128)S(1)}, u32[]{:S(2)}, u32[]{:S(2)}) collective-permute-start(f32[2,3,10,8,2]{4,2,3,1,0:T(8,128)S(1)} %get-tuple-element.26), channel_id=1, source_target_pairs={{0,1},{1,2},{2,3},{4,5},{5,6},{6,7},{8,9},{9,10},{10,11},{12,13},{... | collective-permute-start | bytes 11528 | tf_op jit(solution)/shard_map/ppermute | solution.py:18
  70.6 9.4 %collective-permute-start.9 = (f32[2,3,10,8,2]{4,2,3,1,0:T(8,128)S(1)}, f32[2,3,10,8,2]{4,2,3,1,0:T(8,128)S(1)}, u32[]{:S(2)}, u32[]{:S(2)}) collective-permute-start(f32[2,3,10,8,2]{4,2,3,1,0:T(8,128)S(1)} %get-tuple-element.27), channel_id=1, source_target_pairs={{1,0},{2,1},{3,2},{5,4},{6,5},{7,6},{9,8},{10,9},{11,10},{13,12},{... | collective-permute-start | bytes 11528 | tf_op jit(solution)/shard_map/ppermute | solution.py:20
  86.6 4.5 %collective-permute-start.10 = (f32[2,3,2,8,16]{4,2,3,1,0:T(2,128)S(1)}, f32[2,3,2,8,16]{4,2,3,1,0:T(2,128)S(1)}, u32[]{:S(2)}, u32[]{:S(2)}) collective-permute-start(f32[2,3,2,8,16]{4,2,3,1,0:T(2,128)S(1)} %fusion.51), channel_id=1, source_target_pairs={{0,8},{8,16},{16,24},{1,9},{9,17},{17,25},{2,10},{10,18},{18,26},{... | collective-permute-start | bytes 18440 | tf_op jit(solution)/shard_map/ppermute | solution.py:18
  89.8 4.8 %collective-permute-start.11 = (f32[2,3,2,8,16]{4,2,3,1,0:T(2,128)S(1)}, f32[2,3,2,8,16]{4,2,3,1,0:T(2,128)S(1)}, u32[]{:S(2)}, u32[]{:S(2)}) collective-permute-start(f32[2,3,2,8,16]{4,2,3,1,0:T(2,128)S(1)} %fusion.51), channel_id=1, source_target_pairs={{8,0},{16,8},{24,16},{9,1},{17,9},{25,17},{10,2},{18,10},{26,18},{... | collective-permute-start | bytes 18440 | tf_op jit(solution)/shard_map/ppermute | solution.py:20
  94.8 7.2 %collective-permute-start.12 = (f32[2,3,6,8,2]{4,2,3,1,0:T(8,128)S(1)}, f32[2,3,6,8,2]{4,2,3,1,0:T(8,128)S(1)}, u32[]{:S(2)}, u32[]{:S(2)}) collective-permute-start(f32[2,3,6,8,2]{4,2,3,1,0:T(8,128)S(1)} %get-tuple-element.29), channel_id=1, source_target_pairs={{0,1},{1,2},{2,3},{4,5},{5,6},{6,7},{8,9},{9,10},{10,11},{12,13},{... | collective-permute-start | bytes 6920 | tf_op jit(solution)/shard_map/ppermute | solution.py:18
  99.4 7.0 %collective-permute-start.13 = (f32[2,3,6,8,2]{4,2,3,1,0:T(8,128)S(1)}, f32[2,3,6,8,2]{4,2,3,1,0:T(8,128)S(1)}, u32[]{:S(2)}, u32[]{:S(2)}) collective-permute-start(f32[2,3,6,8,2]{4,2,3,1,0:T(8,128)S(1)} %get-tuple-element.28), channel_id=1, source_target_pairs={{1,0},{2,1},{3,2},{5,4},{6,5},{7,6},{9,8},{10,9},{11,10},{13,12},{... | collective-permute-start | bytes 6920 | tf_op jit(solution)/shard_map/ppermute | solution.py:20
where the time goes:
time: 114 us; the launch traced here: 113 us
  starting transfers between devices  39.2 us (34%)
  waiting for transfers between devices  29.5 us (26%)
  matrix products  19.8 us (17%)
  other arithmetic  12.7 us (11%)
  blocking collectives  5.6 us (5%)
  local copies, waits for them, and re-layouts  5.12 us (4%)
    ppermute x7, starting transfers between devices, extended_2(): lax.ppermute(tail, axis, [(i, (i + 1) % count) for i in range(ends)])  28 us
    ppermute x7, waiting for transfers between devices, extended_2(): lax.ppermute(head, axis, [((i + 1) % count, i) for i in range(ends)])  25.7 us
    ppermute x7, starting transfers between devices, extended_2(): lax.ppermute(head, axis, [((i + 1) % count, i) for i in range(ends)])  11.2 us
    dot_general x1, matrix products, shards(): along_z = jnp.einsum('hcxyz,zk->hcxyk', pushes, table_z, precision=highest)  6.22 us
    dot_general x1, matrix products, shards(): along_y = jnp.einsum('hcxyk,yj->hcxjk', along_z, table_y, precision=highest)  5.91 us
    psum x1, blocking collectives, shards(): summed = lax.psum(canvas, 'gy')  5.6 us
    add x2, other arithmetic, window_sum(): running + lax.slice_in_dim(values, offset, offset + keep_count, axis=whic...  5 us
    ppermute x7, waiting for transfers between devices, extended_2(): lax.ppermute(tail, axis, [(i, (i + 1) % count) for i in range(ends)])  3.85 us
  transfers between devices with their start and end apart: 14, of which 10 were waited for; matrix products, arithmetic and copies ran while one was open for 2% of the time, Pallas kernels for 0%

commit v1 on v0

v1 whole, which is shorter than its diff:
```python
import functools

import jax
import jax.numpy as jnp
from jax import lax
from jax.experimental import pallas as pl
from jax.experimental.pallas import tpu as pltpu
from jax.sharding import PartitionSpec as P

epsilon_value = 1e-05
step_size = 0.5
RAD = 4
MESH = pl.DeviceIdType.MESH
HIGH = lax.Precision.HIGHEST


def beta(offset):
    magnitude = jnp.abs(offset)
    interior = 2.0 / 3.0 - magnitude * magnitude + 0.5 * magnitude * magnitude * magnitude
    outside = jnp.maximum(2.0 - magnitude, 0.0)
    outside = outside * outside * outside / 6.0
    return jnp.where(magnitude < 1.0, interior, outside)


def beta_static(t):
    m = abs(t)
    if m < 1.0:
        return 2.0 / 3.0 - m * m + 0.5 * m * m * m
    return max(2.0 - m, 0.0) ** 3 / 6.0


def iota(shape, dim):
    return lax.broadcasted_iota(jnp.int32, shape, dim)


def lane_groups(lanes, groups, size):
    group = jnp.zeros_like(lanes)
    for n in range(1, groups + 1):
        group = group + (lanes >= n * size).astype(jnp.int32)
    return group, lanes - group * size


def split2(x):
    high = x.astype(jnp.bfloat16)
    low = (x - high.astype(jnp.float32)).astype(jnp.bfloat16)
    return high, low


def split3(x):
    high = x.astype(jnp.bfloat16)
    rest = x - high.astype(jnp.float32)
    mid = rest.astype(jnp.bfloat16)
    low = (rest - mid.astype(jnp.float32)).astype(jnp.bfloat16)
    return high, mid, low


def dot32(a, b):
    return jnp.dot(a, b, preferred_element_type=jnp.float32)


def dot_ones(x, ones_twice):
    high, mid, low = split3(x)
    depth = x.shape[1]
    return dot32(jnp.concatenate([high, mid], axis=1), ones_twice) + dot32(low, ones_twice[:depth])


def dot_split(x, table):
    high, low = split2(x)
    t_high, t_low = split2(table)
    return dot32(
        jnp.concatenate([high, low], axis=1), jnp.concatenate([t_high, t_high], axis=0)
    ) + dot32(high, t_low)


def force_kernel(
    counts, img, vel, w_ref, nv_ref,
    vol, hz, pack, xs, t3, h5, acc, velp, ptile, zrecv, slots, canvas,
    halo_send, halo_recv, z_send, z_recv, p_send, p_recv,
):
    nx, ny, nz = counts
    gx, gy, gz = lax.axis_index("gx"), lax.axis_index("gy"), lax.axis_index("gz")
    _, cx, cy, cz = img.shape
    bx, by, bz = cx // 8, cy // 8, cz // 8
    ly = vel.shape[3]
    wx, wz = bx + 4, bz + 4
    rows = cy + 16
    f32 = jnp.float32

    def exists(index, count, d):
        if d == 0:
            return True
        return index + d < count if d > 0 else index + d >= 0

    def valid(o):
        ok = None
        for index, count, d in zip((gx, gy, gz), counts, o):
            if d != 0:
                here = exists(index, count, d)
                ok = here if ok is None else ok & here
        return ok

    span = (-1, 0, 1)
    offsets = [(a, b, c) for c in span for a in span for b in span if (a, b, c) != (0, 0, 0)]
    offsets.sort(key=lambda o: abs(o[2]))
    peers = [(a, b) for a in range(nx) for b in range(ny) if (a, b) != (0, 0)]

    barrier = pltpu.get_barrier_semaphore()

    def greet(px, py, pz):
        pl.semaphore_signal(
            barrier, inc=1, device_id={"gx": px, "gy": py, "gz": pz}, device_id_type=MESH
        )

    for a, b in peers:
        greet(lax.rem(gx + a, nx), lax.rem(gy + b, ny), gz)
    for o in offsets:
        if o[2] != 0:

            @pl.when(valid(o))
            def _(o=o):
                greet(gx + o[0], gy + o[1], gz + o[2])

    lane = iota((cy, cz), 1)
    cell = lane // RAD
    edge_low = jnp.zeros((cy, cz), f32)
    edge_high = jnp.zeros((cy, cz), f32)
    for g in range(2 * cx):
        v = img[g // cx, g % cx]
        low = pltpu.roll(v, RAD * g, 1) if g else v
        shift = (RAD * g + RAD) % cz
        high = pltpu.roll(v, shift, 1) if shift else v
        edge_low = jnp.where(cell == g, low, edge_low)
        edge_high = jnp.where(cell == g, high, edge_high)
    pack[0] = edge_low
    pack[1] = edge_high

    def sides(index, count):
        return jnp.int32(index > 0) + jnp.int32(index < count - 1)

    beside = (1 + sides(gx, nx)) * (1 + sides(gy, ny)) * sides(gz, nz)
    pl.semaphore_wait(barrier, len(peers) + beside)

    def halo_copy(n, o):
        dx, dy, dz = o
        src_y = {-1: pl.ds(0, 8), 0: pl.ds(0, cy), 1: pl.ds(cy - 8, 8)}[dy]
        dst_y = {-1: pl.ds(cy + 8, 8), 0: pl.ds(8, cy), 1: pl.ds(0, 8)}[dy]
        if dz == 0:
            src_x = {-1: pl.ds(0, RAD), 0: pl.ds(0, cx), 1: pl.ds(cx - RAD, RAD)}[dx]
            dst_x = {-1: pl.ds(cx + RAD, RAD), 0: pl.ds(RAD, cx), 1: pl.ds(0, RAD)}[dx]
            src = img.at[:, src_x, src_y, :]
            dst = vol.at[:, dst_x, dst_y, :]
        else:
            src = pack.at[(dz + 1) // 2, src_y, :]
            dst = hz.at[(1 - dz) // 2, 1 - dx, dst_y, :]
        return pltpu.make_async_remote_copy(
            src_ref=src,
            dst_ref=dst,
            send_sem=halo_send.at[n],
            recv_sem=halo_recv.at[n],
            device_id={"gx": gx + dx, "gy": gy + dy, "gz": gz + dz},
            device_id_type=MESH,
        )

    for n, o in enumerate(offsets):

        @pl.when(valid(o))
        def _(n=n, o=o):
            halo_copy(n, o).start()

    vol[:, RAD : RAD + cx, 8 : 8 + cy, :] = img[...]

    velocity_lane = iota((bz, cz), 1)
    velocity_row = iota((bz, cz), 0)
    take = (iota((8, ly), 1) == by * gy + iota((8, ly), 0) - 2) & (iota((8, ly), 0) >= 2)
    take = (take & (iota((8, ly), 0) < 2 + by)).astype(f32)
    for c in range(6):
        placed = jnp.zeros((ly, cz), f32)
        for i in range(bx):
            spot = (velocity_lane == velocity_row + (2 + i) * wz + 2).astype(f32)
            placed = placed + jnp.dot(
                vel[c // 3, c % 3, i], spot, precision=HIGH, preferred_element_type=f32
            )
        velp[c] = jnp.dot(take, placed, precision=HIGH, preferred_element_type=f32)
    acc[...] = jnp.zeros(acc.shape, f32)

    band = (jnp.abs(iota((cz, cz), 0) - iota((cz, cz), 1)) <= RAD).astype(f32)
    band = jnp.concatenate([band, band], axis=0).astype(jnp.bfloat16)

    def edge_matrix(side, part, image):
        row, col = iota((cz, cz), 0), iota((cz, cz), 1)
        row_x = (row // RAD) % cx + cx * (part - 1)
        dz = row % RAD
        col_x = col // (2 * RAD)
        place = col % (2 * RAD)
        near = (row // (RAD * cx) == image) & (jnp.abs(row_x - col_x) <= RAD)
        if side == 0:
            reach = (place >= RAD) & (place - RAD <= dz)
        else:
            reach = (place < RAD) & (place >= dz)
        return (near & reach).astype(f32)

    edges = []
    for image in range(2):
        whole = jnp.concatenate(
            [edge_matrix(s, p, image) for s in range(2) for p in range(3)], axis=0
        )
        edges.append(jnp.concatenate([whole, whole], axis=0).astype(jnp.bfloat16))

    for n, o in enumerate(offsets):
        back = tuple(-d for d in o)

        @pl.when(valid(back))
        def _(n=n, o=o):
            halo_copy(n, o).wait_recv()

    @pl.when(gx == 0)
    def _():
        vol[:, 0:RAD] = jnp.zeros((2, RAD, rows, cz), f32)
        hz[:, 0] = jnp.zeros((2, rows, cz), f32)

    @pl.when(gx == nx - 1)
    def _():
        vol[:, cx + RAD :] = jnp.zeros((2, RAD, rows, cz), f32)
        hz[:, 2] = jnp.zeros((2, rows, cz), f32)

    @pl.when(gy == 0)
    def _():
        vol[:, :, 0:8] = jnp.zeros((2, cx + 2 * RAD, 8, cz), f32)
        hz[:, :, 0:8] = jnp.zeros((2, 3, 8, cz), f32)

    @pl.when(gy == ny - 1)
    def _():
        vol[:, :, 8 + cy :] = jnp.zeros((2, cx + 2 * RAD, 8, cz), f32)
        hz[:, :, 8 + cy :] = jnp.zeros((2, 3, 8, cz), f32)

    @pl.when(gz == 0)
    def _():
        hz[0] = jnp.zeros((3, rows, cz), f32)

    @pl.when(gz == nz - 1)
    def _():
        hz[1] = jnp.zeros((3, rows, cz), f32)

    def window_rows(count):
        tall = cy + 8
        t3[0:count] = (
            xs[0:count, 4 : 4 + tall] + xs[0:count, 5 : 5 + tall] + xs[0:count, 6 : 6 + tall]
        )
        return t3[0:count, 0:cy] + t3[0:count, 3 : 3 + cy] + t3[0:count, 6 : 6 + cy]

    for s in range(2):
        for p in range(3):
            t = hz[s, p]
            n = s * 3 + p
            xs[n] = t
            xs[6 + n] = t * t
            xs[12 + n] = t * pltpu.roll(t, cz // 2, 1)
    sums = window_rows(18)
    kinds = jnp.concatenate(
        [
            jnp.concatenate([sums[kind * 6 + n] for n in range(6)], axis=1)
            for kind in range(3)
        ],
        axis=0,
    )
    fixed_edge = dot_ones(kinds, edges[0])
    moving_edge = dot_ones(kinds[0 : 2 * cy], edges[1])
    h5[0] = fixed_edge[0:cy]
    h5[1] = moving_edge[0:cy]
    h5[2] = fixed_edge[cy : 2 * cy]
    h5[3] = moving_edge[cy : 2 * cy]
    h5[4] = fixed_edge[2 * cy :]
    h5[5] = jnp.where(
        lane % RAD == RAD - 1, hz[0, 1, 8 : 8 + cy], pltpu.roll(hz[1, 1, 8 : 8 + cy], 2, 1)
    )

    step = 4
    steps = cx // step

    def group(g, carry):
        first = g * step
        fs = [vol[0, first + d] for d in range(step + 8)]
        ms = [vol[1, first + d] for d in range(step + 8)]
        for k in range(5):
            if k == 0:
                a = fs
            elif k == 1:
                a = ms
            elif k == 2:
                a = [f * f for f in fs]
            elif k == 3:
                a = [m * m for m in ms]
            else:
                a = [f * m for f, m in zip(fs, ms)]
            common = a[3] + a[4] + a[5] + (a[6] + a[7] + a[8])
            left2 = a[1] + a[2]
            right2 = a[9] + a[10]
            xs[k * step] = common + (left2 + a[0])
            xs[k * step + 1] = common + (left2 + a[9])
            xs[k * step + 2] = common + (right2 + a[2])
            xs[k * step + 3] = common + (right2 + a[11])
        flat = window_rows(5 * step).reshape(5 * step * cy, cz)
        sums = dot_ones(flat, band).reshape(5, step, cy, cz)
        inner = (lane < RAD) | (lane >= cz - RAD)
        pulls = []
        for s in range(step):
            x = first + s
            shift = lax.rem(2 * cz - RAD - 2 * RAD * x, cz)
            mean = []
            for k in range(5):
                extra = jnp.where(inner, pltpu.roll(h5[k], shift, 1), 0.0)
                mean.append((sums[k, s] + extra) * (1.0 / 729.0))
            m_f, m_m, q_f, q_m, q_fm = mean
            var_f = q_f - m_f * m_f + epsilon_value
            var_m = q_m - m_m * m_m + epsilon_value
            cov = q_fm - m_f * m_m
            slope_f = cov / var_f
            slope_m = cov / var_m
            factor = (2.0 * 0.5 * step_size) * slope_f / var_m
            own_f = vol[0, x + RAD, 8 : 8 + cy]
            own_m = vol[1, x + RAD, 8 : 8 + cy]
            cen_f = own_f - m_f
            cen_m = own_m - m_m
            pull = [factor * (cen_m - slope_f * cen_f), factor * (cen_f - slope_m * cen_m)]
            forces = []
            for h, own in ((0, own_f), (1, own_m)):
                along_x = (
                    vol[h, x + RAD + 1, 8 : 8 + cy] - vol[h, x + RAD - 1, 8 : 8 + cy]
                )
                along_y = vol[h, x + RAD, 9 : 9 + cy] - vol[h, x + RAD, 7 : 7 + cy]
                turn = lax.rem(2 * cz - 3 - RAD * (h * cx + x), cz)
                beyond = pltpu.roll(h5[5], turn, 1)
                above = jnp.where(lane == cz - 1, beyond, pltpu.roll(own, cz - 1, 1))
                below = jnp.where(lane == 0, beyond, pltpu.roll(own, 1, 1))
                forces += [pull[h] * along_x, pull[h] * along_y, pull[h] * (above - below)]
            pulls.append(forces)
        half = lax.rem(g, 2)
        base = g // 2 + half
        for t in range(4):
            weights = []
            for s in range(step):
                low = beta_static(2 - t + (s - 3.5) / 8.0)
                high = beta_static(1 - t + (s + 4 - 3.5) / 8.0)
                weights.append(jnp.where(half == 0, f32(low), f32(high)))
            for c in range(6):
                total = pulls[0][c] * weights[0]
                for s in range(1, step):
                    total = total + pulls[s][c] * weights[s]
                acc[c, base + t] = acc[c, base + t] + total
        return carry

    lax.fori_loop(0, steps, group, 0)

    points_lane = iota((cz, cz), 1)
    _, table_k = lane_groups(points_lane, wx, wz)
    position = iota((cz, cz), 0) - 8 * (table_k - 2)
    table_z = beta((position.astype(f32) - 3.5) / 8.0)
    along = dot_split(acc[...].reshape(6 * wx * cy, cz), table_z).reshape(6, wx, cy, cz)
    lane_i, _ = lane_groups(lane, wx, wz)
    row_j = iota((8, cy), 0)
    table_y = beta((iota((8, cy), 1) - 8 * (row_j - 2)).astype(f32) / 8.0 - 3.5 / 8.0)
    table_y = table_y[: by + 4]
    for c in range(6):
        packed = jnp.zeros((cy, cz), f32)
        for i in range(wx):
            packed = jnp.where(lane_i == i, along[c, i], packed)
        ptile[c] = velp[c] + jnp.dot(
            table_y, packed, precision=HIGH, preferred_element_type=f32
        )

    def z_copy(n):
        d = 1 - 2 * n
        return pltpu.make_async_remote_copy(
            src_ref=ptile,
            dst_ref=zrecv.at[n],
            send_sem=z_send.at[n],
            recv_sem=z_recv.at[n],
            device_id={"gx": gx, "gy": gy, "gz": gz + d},
            device_id_type=MESH,
        )

    for n in range(2):

        @pl.when(exists(gz, nz, 1 - 2 * n))
        def _(n=n):
            z_copy(n).start()

    for n in range(2):
        here = exists(gz, nz, 2 * n - 1)

        @pl.when(here)
        def _(n=n):
            z_copy(n).wait_recv()

        @pl.when(jnp.logical_not(here))
        def _(n=n):
            zrecv[n] = jnp.zeros(ptile.shape, f32)

    tile_rows = 6 * (by + 4)
    tile_lane = iota((tile_rows, cz), 1)
    _, tile_k = lane_groups(tile_lane, wx, wz)
    from_left = pltpu.roll(zrecv[0].reshape(tile_rows, cz), cz - bz, 1)
    from_right = pltpu.roll(zrecv[1].reshape(tile_rows, cz), bz, 1)
    joined = (
        ptile[...].reshape(tile_rows, cz)
        + jnp.where(tile_k < 4, from_left, 0.0)
        + jnp.where(tile_k >= bz, from_right, 0.0)
    )
    me = gx * ny + gy
    slots[me] = joined.reshape(ptile.shape)

    def p_copy(n, a, b):
        return pltpu.make_async_remote_copy(
            src_ref=slots.at[me],
            dst_ref=slots.at[me],
            send_sem=p_send.at[n],
            recv_sem=p_recv.at[n],
            device_id={"gx": lax.rem(gx + a, nx), "gy": lax.rem(gy + b, ny), "gz": gz},
            device_id_type=MESH,
        )

    for n, (a, b) in enumerate(peers):
        p_copy(n, a, b).start()
    canvas[...] = jnp.zeros(canvas.shape, f32)
    for n, (a, b) in enumerate(peers):
        p_copy(n, a, b).wait_recv()

    for a in range(nx):
        for b in range(ny):
            spot = (a, slice(None), slice(by * b, by * b + by + 4))
            canvas[spot] = canvas[spot] + slots[a * ny + b]
    tall = canvas.shape[2]
    flat_lane = iota((6 * tall, cz), 1)
    full = jnp.zeros((6 * tall, cz), f32)
    for a in range(nx):
        move = bx * wz * (a - gx)
        part = pltpu.roll(canvas[a].reshape(6 * tall, cz), lax.rem(move + nx * cz, cz), 1)
        source = flat_lane - move
        full = full + jnp.where((source >= 0) & (source < wx * wz), part, 0.0)
    point_i, point_k = lane_groups(flat_lane, wx, wz)
    global_i = bx * gx - 2 + point_i
    global_k = bz * gz - 2 + point_k
    inside = (flat_lane < wx * wz) & (global_i >= 0) & (global_i < bx * nx)
    inside = inside & (global_k >= 0) & (global_k < bz * nz)
    full = jnp.where(inside, full, 0.0).reshape(6, tall, cz)
    row = iota((6, tall, cz), 1)
    full = jnp.where((row >= 2) & (row < 2 + ly), full, 0.0)
    canvas[0] = full
    for c in range(6):
        for i in range(bx):
            moved = pltpu.roll(canvas[0, c], cz - ((2 + i) * wz + 2), 1)
            nv_ref[c // 3, c % 3, i] = moved[2 : 2 + ly, 0:bz]
    window = canvas[0, :, 0 : by + 4]
    for b in range(1, ny):
        window = jnp.where(gy == b, canvas[0, :, by * b : by * b + by + 4], window)
    w_ref[...] = window

    for n, o in enumerate(offsets):

        @pl.when(valid(o))
        def _(n=n, o=o):
            halo_copy(n, o).wait_send()

    for n in range(2):

        @pl.when(exists(gz, nz, 1 - 2 * n))
        def _(n=n):
            z_copy(n).wait_send()

    for n, (a, b) in enumerate(peers):
        p_copy(n, a, b).wait_send()


def field_kernel(w_ref, out_ref, spread):
    cx, cy, cz = out_ref.shape[2:]
    bx, by, bz = cx // 8, cy // 8, cz // 8
    wx, wz = bx + 4, bz + 4
    wy = by + 4
    f32 = jnp.float32
    row = iota((cz, cz), 0)
    group, place = lane_groups(row, wx, wz)
    table = beta(((iota((cz, cz), 1) - 8 * (place - 2)).astype(f32) - 3.5) / 8.0)
    flat = w_ref[...].reshape(6 * wy, cz)
    lane_i, _ = lane_groups(iota((6 * wy, cz), 1), wx, wz)
    stack = jnp.concatenate([jnp.where(lane_i == i, flat, 0.0) for i in range(wx)], axis=0)
    spread[...] = dot_split(stack, table).reshape(wx, 6, wy, cz)
    sub = (iota((8, cz), 0).astype(f32) - 3.5) / 8.0
    taps = [beta(2.0 - t + sub) for t in range(5)]
    for c in range(6):
        for b in range(by):
            lines = []
            for i in range(wx):
                total = None
                for t in range(5):
                    term = taps[t] * spread[i, c, b + t : b + t + 1]
                    total = term if total is None else total + term
                lines.append(total)
            for x in range(cx):
                block, s = x // 8, x % 8
                half = s // 4
                total = None
                for t in range(half, half + 4):
                    term = beta_static(2 - t + (s - 3.5) / 8.0) * lines[block + t]
                    total = term if total is None else total + term
                out_ref[c // 3, c % 3, x, 8 * b : 8 * b + 8] = total.astype(jnp.bfloat16)


def shards(counts, images, velocity):
    nx, ny, nz = counts
    _, cx, cy, cz = images.shape
    bx, by, bz = cx // 8, cy // 8, cz // 8
    wy = by + 4
    tall = -(-(by * ny + 4) // 8) * 8
    rows = cy + 16
    f32 = jnp.float32
    vmem = pl.BlockSpec(memory_space=pltpu.VMEM)
    offsets = 26
    peers = nx * ny - 1
    window, new_velocity = pl.pallas_call(
        functools.partial(force_kernel, counts),
        out_shape=(
            jax.ShapeDtypeStruct((6, wy, cz), f32),
            jax.ShapeDtypeStruct(velocity.shape, f32),
        ),
        in_specs=[vmem, vmem],
        out_specs=(vmem, vmem),
        scratch_shapes=[
            pltpu.VMEM((2, cx + 2 * RAD, rows, cz), f32),
            pltpu.VMEM((2, 3, rows, cz), f32),
            pltpu.VMEM((2, cy, cz), f32),
            pltpu.VMEM((20, rows, cz), f32),
            pltpu.VMEM((20, cy + 8, cz), f32),
            pltpu.VMEM((6, cy, cz), f32),
            pltpu.VMEM((6, bx + 4, cy, cz), f32),
            pltpu.VMEM((6, wy, cz), f32),
            pltpu.VMEM((6, wy, cz), f32),
            pltpu.VMEM((2, 6, wy, cz), f32),
            pltpu.VMEM((nx * ny, 6, wy, cz), f32),
            pltpu.VMEM((nx, 6, tall, cz), f32),
            pltpu.SemaphoreType.DMA((offsets,)),
            pltpu.SemaphoreType.DMA((offsets,)),
            pltpu.SemaphoreType.DMA((2,)),
            pltpu.SemaphoreType.DMA((2,)),
            pltpu.SemaphoreType.DMA((peers,)),
            pltpu.SemaphoreType.DMA((peers,)),
        ],
        compiler_params=pltpu.CompilerParams(collective_id=0, has_side_effects=True),
        name="forces",
    )(images, velocity)
    field = pl.pallas_call(
        field_kernel,
        out_shape=jax.ShapeDtypeStruct((2, 3, cx, cy, cz), jnp.bfloat16),
        in_specs=[vmem],
        out_specs=vmem,
        scratch_shapes=[pltpu.VMEM((bx + 4, 6, wy, cz), f32)],
        name="field",
    )(window)
    return new_velocity, field


def solution(mesh):
    placed = (P(None, "gx", "gy", "gz"), P(None, None, "gx", None, "gz"))
    counts = tuple(mesh.shape[a] for a in ("gx", "gy", "gz"))
    return jax.shard_map(
        functools.partial(shards, counts),
        mesh=mesh,
        in_specs=placed,
        out_specs=(P(None, None, "gx", None, "gz"), P(None, None, "gx", "gy", "gz")),
        check_vma=False,
    )
```

time: 114 us -> 30.1 us (0.26)
  starting transfers between devices: 39.2 us -> 0 us
  waiting for transfers between devices: 29.5 us -> 0 us
  Pallas kernels: 0 us -> 28.7 us
  matrix products: 19.8 us -> 0 us
  other arithmetic: 12.7 us -> 0 us
  blocking collectives: 5.6 us -> 0 us
  local copies, waits for them, and re-layouts: 5.12 us -> 0.62 us
    ppermute x14 -> x0, starting transfers between devices: 39.2 us -> none  [the longest x7 28 us: extended_2(): lax.ppermute(tail, axis, [(i, (i + 1) % count) for i in range(ends)])]
    ppermute x14 -> x0, waiting for transfers between devices: 29.5 us -> none  [the longest x7 25.7 us: extended_2(): lax.ppermute(head, axis, [((i + 1) % count, i) for i in range(ends)])]
    pallas_call x0 -> x2, Pallas kernels: none -> 28.7 us  [the longest x1 26.2 us: shards(): pl.pallas_call(functools.partial(force_kernel, counts), out_shape=(jax.Sh...]
    dot_general x8 -> x0, matrix products: 19.8 us -> none  [the longest x1 6.22 us: shards(): along_z = jnp.einsum('hcxyz,zk->hcxyk', pushes, table_z, precision=highest)]
    psum x1 -> x0, blocking collectives: 5.6 us -> none  [shards(): summed = lax.psum(canvas, 'gy')]
    add x8 -> x0, other arithmetic: 5.07 us -> none  [the longest x2 5 us: window_sum(): running + lax.slice_in_dim(values, offset, offset + keep_count, axis=whic...]
    div x1 -> x0, other arithmetic: 2.76 us -> none  [local_forces(): averages = window_sums / 729.0]
    slice x8 -> x0, local copies, waits for them, and re-layouts: 2.44 us -> none  [the longest x3 1.48 us: extended_2(): head = lax.slice_in_dim(cells, 0, width, axis=dim)]
  transfers between devices with their start and end apart: 14 -> 0, of which waited for: 10 -> 0; matrix products, arithmetic and copies ran while one was open for 2% -> 0% of each run, Pallas kernels for 0% -> 0%
where the time goes in v1:
time: 30.1 us; the launch traced here: 30 us
  Pallas kernels  28.7 us (95%)
  between operations  0.65 us (2%)
  local copies, waits for them, and re-layouts  0.62 us (2%)
    pallas_call x1, Pallas kernels, shards(): pl.pallas_call(functools.partial(force_kernel, counts), out_shape=(jax.Sh...  26.2 us
    pallas_call x1, Pallas kernels, shards(): pl.pallas_call(field_kernel, out_shape=jax.ShapeDtypeStruct((2, 3, cx, cy...  2.44 us
    unnamed x3, local copies, waits for them, and re-layouts  0.62 us

profile of v1, /device:TPU:1, one launch (start us, length us, event | category | flops | bytes accessed | tf_op | source)
XLA Modules:
  0.0 30.0 jit_solution(14624772165148658341)
XLA Ops:
  0.6 26.2 %forces.1 = (f32[6,8,128]{2,1,0:T(8,128)}, f32[2,3,2,8,16]{4,3,2,1,0:T(8,128)}) custom-call(f32[2,16,32,128]{3,2,1,0:T(8,128)} %img.1, f32[2,3,2,8,16]{4,3,2,1,0:T(8,128)} %vel.1), custom_call_target="tpu_custom_call" | custom-call | tf_op jit(solution)/shard_map/forces/pallas_call | solution.py:519
  26.9 0.0 copy-start
  26.9 2.4 %field.1 = bf16[2,3,16,32,128]{4,3,2,1,0:T(8,128)(2,1)} custom-call(f32[6,8,128]{2,1,0:T(8,128)} %get-tuple-element.5.w_ref), custom_call_target="tpu_custom_call" | custom-call | tf_op jit(solution)/shard_map/field/pallas_call | solution.py:550
  29.3 0.0 copy-done
  29.3 0.6 %copy.5 = f32[2,3,2,8,16]{4,3,2,1,0:T(8,128)} copy(f32[2,3,2,8,16]{4,3,2,1,0:T(8,128)S(1)} %copy-done) | data formatting | bytes 12288
Async XLA Ops:
  26.9 2.5 %copy-start = (f32[2,3,2,8,16]{4,3,2,1,0:T(8,128)S(1)}, f32[2,3,2,8,16]{4,3,2,1,0:T(8,128)}, u32[]{:S(2)}) copy-start(f32[2,3,2,8,16]{4,3,2,1,0:T(8,128)} %get-tuple-element.8) | copy-start | bytes 18436

commit v2 on v1

--- a/solution.py
+++ b/solution.py
@@ -73,13 +73,13 @@
 
 
 def force_kernel(
-    counts, img, vel, w_ref, nv_ref,
-    vol, hz, pack, xs, t3, h5, acc, velp, ptile, zrecv, slots, canvas,
-    halo_send, halo_recv, z_send, z_recv, p_send, p_recv,
+    counts, dims, img_hbm, vel_hbm, w_ref, own_ref,
+    vol, vel, hz, pack, xs, t3, h5, acc, velp, ptile, joined, zrecv, slots, canvas,
+    load, halo_send, halo_recv, z_send, z_recv, p_send, p_recv,
 ):
     nx, ny, nz = counts
     gx, gy, gz = lax.axis_index("gx"), lax.axis_index("gy"), lax.axis_index("gz")
-    _, cx, cy, cz = img.shape
+    cx, cy, cz = dims
     bx, by, bz = cx // 8, cy // 8, cz // 8
     ly = vel.shape[3]
     wx, wz = bx + 4, bz + 4
@@ -102,7 +102,13 @@
     span = (-1, 0, 1)
     offsets = [(a, b, c) for c in span for a in span for b in span if (a, b, c) != (0, 0, 0)]
     offsets.sort(key=lambda o: abs(o[2]))
-    peers = [(a, b) for a in range(nx) for b in range(ny) if (a, b) != (0, 0)]
+    peers = plane_peers(counts, bx)
+
+    img = vol.at[:, RAD : RAD + cx, 8 : 8 + cy, :]
+    load_images = pltpu.make_async_copy(img_hbm, img, load.at[0])
+    load_velocity = pltpu.make_async_copy(vel_hbm, vel, load.at[1])
+    load_images.start()
+    load_velocity.start()
 
     barrier = pltpu.get_barrier_semaphore()
 
@@ -111,21 +117,29 @@
             barrier, inc=1, device_id={"gx": px, "gy": py, "gz": pz}, device_id_type=MESH
         )
 
-    for a, b in peers:
-        greet(lax.rem(gx + a, nx), lax.rem(gy + b, ny), gz)
-    for o in offsets:
-        if o[2] != 0:
-
-            @pl.when(valid(o))
-            def _(o=o):
-                greet(gx + o[0], gy + o[1], gz + o[2])
+    plane = [o for o in offsets if o[2] == 0]
+    if ny > 2:
+        plane = []
+        for d, r in peers:
+
+            @pl.when(True if d == 0 else exists(gx, nx, d))
+            def _(d=d, r=r):
+                greet(gx + d, lax.rem(gy + r, ny), gz)
+
+    for o in plane + [o for o in offsets if o[2] != 0]:
+
+        @pl.when(valid(o))
+        def _(o=o):
+            greet(gx + o[0], gy + o[1], gz + o[2])
+
+    load_images.wait()
 
     lane = iota((cy, cz), 1)
     cell = lane // RAD
     edge_low = jnp.zeros((cy, cz), f32)
     edge_high = jnp.zeros((cy, cz), f32)
     for g in range(2 * cx):
-        v = img[g // cx, g % cx]
+        v = vol[g // cx, RAD + g % cx, 8 : 8 + cy]
         low = pltpu.roll(v, RAD * g, 1) if g else v
         shift = (RAD * g + RAD) % cz
         high = pltpu.roll(v, shift, 1) if shift else v
@@ -137,20 +151,25 @@
     def sides(index, count):
         return jnp.int32(index > 0) + jnp.int32(index < count - 1)
 
-    beside = (1 + sides(gx, nx)) * (1 + sides(gy, ny)) * sides(gz, nz)
-    pl.semaphore_wait(barrier, len(peers) + beside)
+    near = (1 + sides(gx, nx)) * (1 + sides(gy, ny))
+    beside = near * sides(gz, nz)
+    if ny > 2:
+        near = 0
+        for d in sorted({d for d, _ in peers}):
+            near = near + (ny if d == 0 else ny * jnp.int32(exists(gx, nx, d)))
+    pl.semaphore_wait(barrier, near - 1 + beside)
 
     def halo_copy(n, o):
         dx, dy, dz = o
-        src_y = {-1: pl.ds(0, 8), 0: pl.ds(0, cy), 1: pl.ds(cy - 8, 8)}[dy]
-        dst_y = {-1: pl.ds(cy + 8, 8), 0: pl.ds(8, cy), 1: pl.ds(0, 8)}[dy]
+        src_y = {-1: (0, RAD), 0: (0, cy), 1: (cy - RAD, RAD)}[dy]
+        dst_y = {-1: pl.ds(cy + 8, RAD), 0: pl.ds(8, cy), 1: pl.ds(8 - RAD, RAD)}[dy]
         if dz == 0:
-            src_x = {-1: pl.ds(0, RAD), 0: pl.ds(0, cx), 1: pl.ds(cx - RAD, RAD)}[dx]
+            src_x = {-1: pl.ds(RAD, RAD), 0: pl.ds(RAD, cx), 1: pl.ds(cx, RAD)}[dx]
             dst_x = {-1: pl.ds(cx + RAD, RAD), 0: pl.ds(RAD, cx), 1: pl.ds(0, RAD)}[dx]
-            src = img.at[:, src_x, src_y, :]
+            src = vol.at[:, src_x, pl.ds(8 + src_y[0], src_y[1]), :]
             dst = vol.at[:, dst_x, dst_y, :]
         else:
-            src = pack.at[(dz + 1) // 2, src_y, :]
+            src = pack.at[(dz + 1) // 2, pl.ds(*src_y), :]
             dst = hz.at[(1 - dz) // 2, 1 - dx, dst_y, :]
         return pltpu.make_async_remote_copy(
             src_ref=src,
@@ -167,20 +186,19 @@
         def _(n=n, o=o):
             halo_copy(n, o).start()
 
-    vol[:, RAD : RAD + cx, 8 : 8 + cy, :] = img[...]
-
+    load_velocity.wait()
     velocity_lane = iota((bz, cz), 1)
     velocity_row = iota((bz, cz), 0)
     take = (iota((8, ly), 1) == by * gy + iota((8, ly), 0) - 2) & (iota((8, ly), 0) >= 2)
     take = (take & (iota((8, ly), 0) < 2 + by)).astype(f32)
-    for c in range(6):
+    for i in range(bx):
         placed = jnp.zeros((ly, cz), f32)
-        for i in range(bx):
-            spot = (velocity_lane == velocity_row + (2 + i) * wz + 2).astype(f32)
+        for c in range(6):
+            spot = (velocity_lane == velocity_row + c * wz + 2).astype(f32)
             placed = placed + jnp.dot(
                 vel[c // 3, c % 3, i], spot, precision=HIGH, preferred_element_type=f32
             )
-        velp[c] = jnp.dot(take, placed, precision=HIGH, preferred_element_type=f32)
+        velp[i] = jnp.dot(take, placed, precision=HIGH, preferred_element_type=f32)
     acc[...] = jnp.zeros(acc.shape, f32)
 
     band = (jnp.abs(iota((cz, cz), 0) - iota((cz, cz), 1)) <= RAD).astype(f32)
@@ -199,19 +217,23 @@
             reach = (place < RAD) & (place >= dz)
         return (near & reach).astype(f32)
 
-    edges = []
-    for image in range(2):
+    def edge_table(parts, image):
         whole = jnp.concatenate(
-            [edge_matrix(s, p, image) for s in range(2) for p in range(3)], axis=0
-        )
-        edges.append(jnp.concatenate([whole, whole], axis=0).astype(jnp.bfloat16))
-
-    for n, o in enumerate(offsets):
-        back = tuple(-d for d in o)
-
-        @pl.when(valid(back))
-        def _(n=n, o=o):
-            halo_copy(n, o).wait_recv()
+            [edge_matrix(s, p, image) for s in range(2) for p in parts], axis=0
+        )
+        return jnp.concatenate([whole, whole], axis=0).astype(jnp.bfloat16)
+
+    middle = (1,)
+    outer = (0, 2)
+    tables = {parts: [edge_table(parts, n) for n in range(2)] for parts in (middle, outer)}
+
+    def arrive(wanted):
+        for n, o in enumerate(offsets):
+            if (o[0] != 0) == wanted:
+
+                @pl.when(valid(tuple(-d for d in o)))
+                def _(n=n, o=o):
+                    halo_copy(n, o).wait_recv()
 
     @pl.when(gx == 0)
     def _():
@@ -248,28 +270,36 @@
         )
         return t3[0:count, 0:cy] + t3[0:count, 3 : 3 + cy] + t3[0:count, 6 : 6 + cy]
 
-    for s in range(2):
-        for p in range(3):
-            t = hz[s, p]
-            n = s * 3 + p
-            xs[n] = t
-            xs[6 + n] = t * t
-            xs[12 + n] = t * pltpu.roll(t, cz // 2, 1)
-    sums = window_rows(18)
-    kinds = jnp.concatenate(
-        [
-            jnp.concatenate([sums[kind * 6 + n] for n in range(6)], axis=1)
-            for kind in range(3)
-        ],
-        axis=0,
-    )
-    fixed_edge = dot_ones(kinds, edges[0])
-    moving_edge = dot_ones(kinds[0 : 2 * cy], edges[1])
-    h5[0] = fixed_edge[0:cy]
-    h5[1] = moving_edge[0:cy]
-    h5[2] = fixed_edge[cy : 2 * cy]
-    h5[3] = moving_edge[cy : 2 * cy]
-    h5[4] = fixed_edge[2 * cy :]
+    def edge_sums(parts):
+        count = 2 * len(parts)
+        for s in range(2):
+            for m, p in enumerate(parts):
+                t = hz[s, p]
+                n = s * len(parts) + m
+                xs[n] = t
+                xs[count + n] = t * t
+                xs[2 * count + n] = t * pltpu.roll(t, cz // 2, 1)
+        sums = window_rows(3 * count)
+        kinds = jnp.concatenate(
+            [
+                jnp.concatenate([sums[kind * count + n] for n in range(count)], axis=1)
+                for kind in range(3)
+            ],
+            axis=0,
+        )
+        fixed_edge = dot_ones(kinds, tables[parts][0])
+        moving_edge = dot_ones(kinds[0 : 2 * cy], tables[parts][1])
+        return [
+            fixed_edge[0:cy],
+            moving_edge[0:cy],
+            fixed_edge[cy : 2 * cy],
+            moving_edge[cy : 2 * cy],
+            fixed_edge[2 * cy :],
+        ]
+
+    arrive(False)
+    for k, value in enumerate(edge_sums(middle)):
+        h5[k] = value
     h5[5] = jnp.where(
         lane % RAD == RAD - 1, hz[0, 1, 8 : 8 + cy], pltpu.roll(hz[1, 1, 8 : 8 + cy], 2, 1)
     )
@@ -349,24 +379,30 @@
                 acc[c, base + t] = acc[c, base + t] + total
         return carry
 
-    lax.fori_loop(0, steps, group, 0)
+    lax.fori_loop(1, steps - 1, group, 0)
+    arrive(True)
+    for k, value in enumerate(edge_sums(outer)):
+        h5[k] = h5[k] + value
+    lax.fori_loop(0, 2, lambda n, carry: group(n * (steps - 1), carry), 0)
 
     points_lane = iota((cz, cz), 1)
-    _, table_k = lane_groups(points_lane, wx, wz)
+    _, table_k = lane_groups(points_lane, 6, wz)
     position = iota((cz, cz), 0) - 8 * (table_k - 2)
     table_z = beta((position.astype(f32) - 3.5) / 8.0)
     along = dot_split(acc[...].reshape(6 * wx * cy, cz), table_z).reshape(6, wx, cy, cz)
-    lane_i, _ = lane_groups(lane, wx, wz)
+    lane_c, _ = lane_groups(lane, 6, wz)
     row_j = iota((8, cy), 0)
     table_y = beta((iota((8, cy), 1) - 8 * (row_j - 2)).astype(f32) / 8.0 - 3.5 / 8.0)
     table_y = table_y[: by + 4]
-    for c in range(6):
+    for i in range(wx):
         packed = jnp.zeros((cy, cz), f32)
-        for i in range(wx):
-            packed = jnp.where(lane_i == i, along[c, i], packed)
-        ptile[c] = velp[c] + jnp.dot(
+        for c in range(6):
+            packed = jnp.where(lane_c == c, along[c, i], packed)
+        ptile[i] = jnp.dot(
             table_y, packed, precision=HIGH, preferred_element_type=f32
         )
+        if 2 <= i < 2 + bx:
+            ptile[i] = ptile[i] + velp[i - 2]
 
     def z_copy(n):
         d = 1 - 2 * n
@@ -396,63 +432,69 @@
         def _(n=n):
             zrecv[n] = jnp.zeros(ptile.shape, f32)
 
-    tile_rows = 6 * (by + 4)
+    tile_rows = wx * (by + 4)
     tile_lane = iota((tile_rows, cz), 1)
-    _, tile_k = lane_groups(tile_lane, wx, wz)
+    _, tile_k = lane_groups(tile_lane, 6, wz)
     from_left = pltpu.roll(zrecv[0].reshape(tile_rows, cz), cz - bz, 1)
     from_right = pltpu.roll(zrecv[1].reshape(tile_rows, cz), bz, 1)
-    joined = (
+    total = (
         ptile[...].reshape(tile_rows, cz)
         + jnp.where(tile_k < 4, from_left, 0.0)
         + jnp.where(tile_k >= bz, from_right, 0.0)
     )
-    me = gx * ny + gy
-    slots[me] = joined.reshape(ptile.shape)
-
-    def p_copy(n, a, b):
+    joined[...] = total.reshape(ptile.shape)
+    far = max(d for d, _ in peers)
+
+    def shared(d):
+        here = max(0, bx * d)
+        there = max(0, -bx * d)
+        return here, there, wx - bx * abs(d)
+
+    def p_copy(n, d, r):
+        here, there, size = shared(d)
         return pltpu.make_async_remote_copy(
-            src_ref=slots.at[me],
-            dst_ref=slots.at[me],
+            src_ref=joined.at[pl.ds(here, size)],
+            dst_ref=slots.at[far + d, gy, pl.ds(there, size)],
             send_sem=p_send.at[n],
             recv_sem=p_recv.at[n],
-            device_id={"gx": lax.rem(gx + a, nx), "gy": lax.rem(gy + b, ny), "gz": gz},
+            device_id={"gx": gx + d, "gy": lax.rem(gy + r, ny), "gz": gz},
             device_id_type=MESH,
         )
 
-    for n, (a, b) in enumerate(peers):
-        p_copy(n, a, b).start()
+    for n, (d, r) in enumerate(peers):
+
+        @pl.when(True if d == 0 else exists(gx, nx, d))
+        def _(n=n, d=d, r=r):
+            p_copy(n, d, r).start()
+
+    slots[far, gy] = joined[...]
     canvas[...] = jnp.zeros(canvas.shape, f32)
-    for n, (a, b) in enumerate(peers):
-        p_copy(n, a, b).wait_recv()
-
-    for a in range(nx):
-        for b in range(ny):
-            spot = (a, slice(None), slice(by * b, by * b + by + 4))
-            canvas[spot] = canvas[spot] + slots[a * ny + b]
-    tall = canvas.shape[2]
-    flat_lane = iota((6 * tall, cz), 1)
-    full = jnp.zeros((6 * tall, cz), f32)
-    for a in range(nx):
-        move = bx * wz * (a - gx)
-        part = pltpu.roll(canvas[a].reshape(6 * tall, cz), lax.rem(move + nx * cz, cz), 1)
-        source = flat_lane - move
-        full = full + jnp.where((source >= 0) & (source < wx * wz), part, 0.0)
-    point_i, point_k = lane_groups(flat_lane, wx, wz)
-    global_i = bx * gx - 2 + point_i
+    for d in sorted({d for d, _ in peers}, key=abs):
+
+        @pl.when(True if d == 0 else exists(gx, nx, -d))
+        def _(d=d):
+            for n, (e, r) in enumerate(peers):
+                if e == d:
+                    p_copy(n, d, r).wait_recv()
+            _, there, size = shared(d)
+            for b in range(ny):
+                spot = (slice(there, there + size), slice(by * b, by * b + by + 4))
+                canvas[spot] = canvas[spot] + slots[far + d, b, there : there + size]
+
+    tall = canvas.shape[1]
+    shape = (wx, tall, cz)
+    point_c, point_k = lane_groups(iota(shape, 2), 6, wz)
+    global_i = bx * gx - 2 + iota(shape, 0)
     global_k = bz * gz - 2 + point_k
-    inside = (flat_lane < wx * wz) & (global_i >= 0) & (global_i < bx * nx)
+    row = iota(shape, 1)
+    inside = (point_c < 6) & (global_i >= 0) & (global_i < bx * nx)
     inside = inside & (global_k >= 0) & (global_k < bz * nz)
-    full = jnp.where(inside, full, 0.0).reshape(6, tall, cz)
-    row = iota((6, tall, cz), 1)
-    full = jnp.where((row >= 2) & (row < 2 + ly), full, 0.0)
-    canvas[0] = full
-    for c in range(6):
-        for i in range(bx):
-            moved = pltpu.roll(canvas[0, c], cz - ((2 + i) * wz + 2), 1)
-            nv_ref[c // 3, c % 3, i] = moved[2 : 2 + ly, 0:bz]
-    window = canvas[0, :, 0 : by + 4]
+    inside = inside & (row >= 2) & (row < 2 + ly)
+    canvas[...] = jnp.where(inside, canvas[...], 0.0)
+    own_ref[...] = canvas[2 : 2 + bx]
+    window = canvas[:, 0 : by + 4]
     for b in range(1, ny):
-        window = jnp.where(gy == b, canvas[0, :, by * b : by * b + by + 4], window)
+        window = jnp.where(gy == b, canvas[:, by * b : by * b + by + 4], window)
     w_ref[...] = window
 
     for n, o in enumerate(offsets):
@@ -467,23 +509,34 @@
         def _(n=n):
             z_copy(n).wait_send()
 
-    for n, (a, b) in enumerate(peers):
-        p_copy(n, a, b).wait_send()
-
-
-def field_kernel(w_ref, out_ref, spread):
-    cx, cy, cz = out_ref.shape[2:]
+    for n, (d, r) in enumerate(peers):
+
+        @pl.when(True if d == 0 else exists(gx, nx, d))
+        def _(n=n, d=d, r=r):
+            p_copy(n, d, r).wait_send()
+
+
+def plane_peers(counts, bx):
+    nx, ny, _ = counts
+    far = min(nx - 1, (bx + 3) // bx)
+    pairs = [(d, r) for d in range(-far, far + 1) for r in range(ny)]
+    return [pair for pair in pairs if pair != (0, 0)]
+
+
+def field_kernel(w_ref, own_ref, nv_ref, out_hbm, spread, held, done):
+    cx, cy, cz = held.shape[1:]
+    ly = nv_ref.shape[3]
     bx, by, bz = cx // 8, cy // 8, cz // 8
     wx, wz = bx + 4, bz + 4
     wy = by + 4
     f32 = jnp.float32
     row = iota((cz, cz), 0)
-    group, place = lane_groups(row, wx, wz)
+    group, place = lane_groups(row, 6, wz)
     table = beta(((iota((cz, cz), 1) - 8 * (place - 2)).astype(f32) - 3.5) / 8.0)
-    flat = w_ref[...].reshape(6 * wy, cz)
-    lane_i, _ = lane_groups(iota((6 * wy, cz), 1), wx, wz)
-    stack = jnp.concatenate([jnp.where(lane_i == i, flat, 0.0) for i in range(wx)], axis=0)
-    spread[...] = dot_split(stack, table).reshape(wx, 6, wy, cz)
+    flat = w_ref[...].reshape(wx * wy, cz)
+    lane_c, _ = lane_groups(iota((wx * wy, cz), 1), 6, wz)
+    stack = jnp.concatenate([jnp.where(lane_c == c, flat, 0.0) for c in range(6)], axis=0)
+    spread[...] = dot_split(stack, table).reshape(6, wx, wy, cz)
     sub = (iota((8, cz), 0).astype(f32) - 3.5) / 8.0
     taps = [beta(2.0 - t + sub) for t in range(5)]
     for c in range(6):
@@ -492,7 +545,7 @@
             for i in range(wx):
                 total = None
                 for t in range(5):
-                    term = taps[t] * spread[i, c, b + t : b + t + 1]
+                    term = taps[t] * spread[c, i, b + t : b + t + 1]
                     total = term if total is None else total + term
                 lines.append(total)
             for x in range(cx):
@@ -502,7 +555,15 @@
                 for t in range(half, half + 4):
                     term = beta_static(2 - t + (s - 3.5) / 8.0) * lines[block + t]
                     total = term if total is None else total + term
-                out_ref[c // 3, c % 3, x, 8 * b : 8 * b + 8] = total.astype(jnp.bfloat16)
+                held[c, x, 8 * b : 8 * b + 8] = total.astype(jnp.bfloat16)
+        pltpu.make_async_copy(held.at[c], out_hbm.at[c // 3, c % 3], done.at[c]).start()
+    for i in range(bx):
+        for c in range(6):
+            moved = own_ref[i]
+            moved = pltpu.roll(moved, cz - (c * wz + 2), 1)
+            nv_ref[c // 3, c % 3, i] = moved[2 : 2 + ly, 0:bz]
+    for c in range(6):
+        pltpu.make_async_copy(held.at[c], out_hbm.at[c // 3, c % 3], done.at[c]).wait()
 
 
 def shards(counts, images, velocity):
@@ -514,47 +575,60 @@
     rows = cy + 16
     f32 = jnp.float32
     vmem = pl.BlockSpec(memory_space=pltpu.VMEM)
+    hbm = pl.BlockSpec(memory_space=pl.ANY)
     offsets = 26
-    peers = nx * ny - 1
-    window, new_velocity = pl.pallas_call(
-        functools.partial(force_kernel, counts),
+    peers = plane_peers(counts, bx)
+    far = max(d for d, _ in peers)
+    wx = bx + 4
+    window, own = pl.pallas_call(
+        functools.partial(force_kernel, counts, (cx, cy, cz)),
         out_shape=(
-            jax.ShapeDtypeStruct((6, wy, cz), f32),
-            jax.ShapeDtypeStruct(velocity.shape, f32),
+            jax.ShapeDtypeStruct((wx, wy, cz), f32),
+            jax.ShapeDtypeStruct((bx, tall, cz), f32),
         ),
-        in_specs=[vmem, vmem],
+        in_specs=[hbm, hbm],
         out_specs=(vmem, vmem),
         scratch_shapes=[
             pltpu.VMEM((2, cx + 2 * RAD, rows, cz), f32),
+            pltpu.VMEM(velocity.shape, f32),
             pltpu.VMEM((2, 3, rows, cz), f32),
             pltpu.VMEM((2, cy, cz), f32),
             pltpu.VMEM((20, rows, cz), f32),
             pltpu.VMEM((20, cy + 8, cz), f32),
             pltpu.VMEM((6, cy, cz), f32),
-            pltpu.VMEM((6, bx + 4, cy, cz), f32),
-            pltpu.VMEM((6, wy, cz), f32),
-            pltpu.VMEM((6, wy, cz), f32),
-            pltpu.VMEM((2, 6, wy, cz), f32),
-            pltpu.VMEM((nx * ny, 6, wy, cz), f32),
-            pltpu.VMEM((nx, 6, tall, cz), f32),
+            pltpu.VMEM((6, wx, cy, cz), f32),
+            pltpu.VMEM((bx, wy, cz), f32),
+            pltpu.VMEM((wx, wy, cz), f32),
+            pltpu.VMEM((wx, wy, cz), f32),
+            pltpu.VMEM((2, wx, wy, cz), f32),
+            pltpu.VMEM((2 * far + 1, ny, wx, wy, cz), f32),
+            pltpu.VMEM((wx, tall, cz), f32),
+            pltpu.SemaphoreType.DMA((2,)),
             pltpu.SemaphoreType.DMA((offsets,)),
             pltpu.SemaphoreType.DMA((offsets,)),
             pltpu.SemaphoreType.DMA((2,)),
             pltpu.SemaphoreType.DMA((2,)),
-            pltpu.SemaphoreType.DMA((peers,)),
-            pltpu.SemaphoreType.DMA((peers,)),
+            pltpu.SemaphoreType.DMA((len(peers),)),
+            pltpu.SemaphoreType.DMA((len(peers),)),
         ],
         compiler_params=pltpu.CompilerParams(collective_id=0, has_side_effects=True),
         name="forces",
     )(images, velocity)
-    field = pl.pallas_call(
+    new_velocity, field = pl.pallas_call(
         field_kernel,
-        out_shape=jax.ShapeDtypeStruct((2, 3, cx, cy, cz), jnp.bfloat16),
-        in_specs=[vmem],
-        out_specs=vmem,
-        scratch_shapes=[pltpu.VMEM((bx + 4, 6, wy, cz), f32)],
+        out_shape=(
+            jax.ShapeDtypeStruct(velocity.shape, f32),
+            jax.ShapeDtypeStruct((2, 3, cx, cy, cz), jnp.bfloat16),
+        ),
+        in_specs=[vmem, vmem],
+        out_specs=(vmem, hbm),
+        scratch_shapes=[
+            pltpu.VMEM((6, wx, wy, cz), f32),
+            pltpu.VMEM((6, cx, cy, cz), jnp.bfloat16),
+            pltpu.SemaphoreType.DMA((6,)),
+        ],
         name="field",
-    )(window)
+    )(window, own)
     return new_velocity, field
 
 

time: 30.1 us -> 25.3 us (0.84)
  Pallas kernels: 28.7 us -> 24.5 us
  local copies, waits for them, and re-layouts: 0.62 us -> 0 us
    pallas_call x2, Pallas kernels: 28.7 us -> 24.5 us  [the longest x1 21.5 us: shards(): pl.pallas_call(functools.partial(force_kernel, counts, (cx, cy, cz)), out...]
    unnamed x3 -> x0, local copies, waits for them, and re-layouts: 0.62 us -> none
where the time goes in v2:
time: 25.3 us; the launch traced here: 25.1 us
  Pallas kernels  24.5 us (97%)
  between operations  0.64 us (3%)
    pallas_call x1, Pallas kernels, shards(): pl.pallas_call(functools.partial(force_kernel, counts, (cx, cy, cz)), out...  21.5 us
    pallas_call x1, Pallas kernels, shards(): pl.pallas_call(field_kernel, out_shape=(jax.ShapeDtypeStruct(velocity.sha...  2.95 us

profile of v2, /device:TPU:1, one launch (start us, length us, event | category | flops | bytes accessed | tf_op | source)
XLA Modules:
  0.0 25.1 jit_solution(17637322817925610908)
XLA Ops:
  0.6 21.5 %forces.1 = (f32[6,8,128]{2,1,0:T(8,128)}, f32[2,16,128]{2,1,0:T(8,128)}) custom-call(f32[2,16,32,128]{3,2,1,0:T(8,128)} %img_hbm.1, f32[2,3,2,8,16]{4,3,2,1,0:T(8,128)} %vel_hbm.1), custom_call_target="tpu_custom_call" | custom-call | tf_op jit(solution)/shard_map/forces/pallas_call | solution.py:583
  22.1 3.0 %field.1 = (f32[2,3,2,8,16]{4,3,2,1,0:T(8,128)}, bf16[2,3,16,32,128]{4,3,2,1,0:T(8,128)(2,1)}) custom-call(f32[6,8,128]{2,1,0:T(8,128)} %get-tuple-element.4.w_ref, f32[2,16,128]{2,1,0:T(8,128)} %get-tuple-element.5.own_ref), custom_call_target="tpu_custom_call" | custom-call | tf_op jit(solution)/shard_map/field/pallas_call | solution.py:617

commit v3 on v2

--- a/solution.py
+++ b/solution.py
@@ -583,8 +583,8 @@
     window, own = pl.pallas_call(
         functools.partial(force_kernel, counts, (cx, cy, cz)),
         out_shape=(
-            jax.ShapeDtypeStruct((wx, wy, cz), f32),
-            jax.ShapeDtypeStruct((bx, tall, cz), f32),
+            pltpu.VMEM((wx, wy, cz), f32),
+            pltpu.VMEM((bx, tall, cz), f32),
         ),
         in_specs=[hbm, hbm],
         out_specs=(vmem, vmem),
@@ -628,7 +628,10 @@
             pltpu.SemaphoreType.DMA((6,)),
         ],
         name="field",
-    )(window, own)
+    )(
+        pltpu.with_memory_space_constraint(window, pltpu.VMEM),
+        pltpu.with_memory_space_constraint(own, pltpu.VMEM),
+    )
     return new_velocity, field
 
 

time: 25.3 us -> 23.9 us (0.945)
  Pallas kernels: 24.5 us -> 23.1 us
    pallas_call x1, Pallas kernels: 2.95 us -> 2.22 us  [shards(): pl.pallas_call(field_kernel, out_shape=(jax.ShapeDtypeStruct(velocity.sha...]
    pallas_call x1, Pallas kernels: 21.5 us -> 20.9 us  [shards(): pl.pallas_call(functools.partial(force_kernel, counts, (cx, cy, cz)), out...]
where the time goes in v3:
time: 23.9 us; the launch traced here: 23.7 us
  Pallas kernels  23.1 us (97%)
  between operations  0.64 us (3%)
    pallas_call x1, Pallas kernels, shards(): pl.pallas_call(functools.partial(force_kernel, counts, (cx, cy, cz)), out...  20.9 us
    pallas_call x1, Pallas kernels, shards(): pl.pallas_call(field_kernel, out_shape=(jax.ShapeDtypeStruct(velocity.sha...  2.22 us

profile of v3, /device:TPU:1, one launch (start us, length us, event | category | flops | bytes accessed | tf_op | source)
XLA Modules:
  0.0 23.7 jit_solution(13318946556407964733)
XLA Ops:
  0.6 20.9 %forces.1 = (f32[6,8,128]{2,1,0:T(8,128)S(1)}, f32[2,16,128]{2,1,0:T(8,128)S(1)}) custom-call(f32[2,16,32,128]{3,2,1,0:T(8,128)} %img_hbm.1, f32[2,3,2,8,16]{4,3,2,1,0:T(8,128)} %vel_hbm.1), custom_call_target="tpu_custom_call" | custom-call | tf_op jit(solution)/shard_map/forces/pallas_call | solution.py:583
  21.5 2.2 %field.1 = (f32[2,3,2,8,16]{4,3,2,1,0:T(8,128)}, bf16[2,3,16,32,128]{4,3,2,1,0:T(8,128)(2,1)}) custom-call(f32[6,8,128]{2,1,0:T(8,128)S(1)} %get-tuple-element.4.w_ref, f32[2,16,128]{2,1,0:T(8,128)S(1)} %get-tuple-element.5.own_ref), custom_call_target="tpu_custom_call" | custom-call | tf_op jit(solution)/shard_map/field/pallas_call | solution.py:617
